TPU v7x, 32 devices: a whole 2x2x4 slice. The times are simulated.
32 devices in a mesh: freq: 2 (over core), row: 4 (over y, x), col: 4 (over z).
Axes of the slice: x: 2, y: 2, z: 4, core: 2. Of those that a mesh axis runs over, the one named last changes fastest.
Arguments:
- coupling: bfloat16 [6144, 6144], P('row', 'col'), may hold values from -0.15625 to 0.15625
- freq_weight: float32 [12288], P(('freq', 'row')), parts along dimension 0, may hold values from 0.05 to 2
Outputs:
- response: float32 [12288, 6144], P(('freq', 'row'), 'col'), parts along dimension 0
There are 2 independent parts, one for each index of `freq`. A program takes and returns all parts, laid end to end along the dimension named above; an argument that names none is the same for every part. Nothing has to cross between parts.
All inputs are finite; a program needn't handle non-finite values.
Results may differ from a plain program's by a relative error of at most 0.0021.
Values may be sent and summed in bfloat16 or wider, within the bound.
A program may use at most 128 MiB of HBM per device.

v0:
```python
import jax
import jax.numpy as jnp
from jax import lax
from jax.sharding import PartitionSpec as P


def on_device(coupling, freq_weight):
    weighted = (coupling.astype(jnp.float32) * freq_weight[:, None]).astype(jnp.bfloat16)
    full_rows = lax.all_gather(weighted, "col", axis=1, tiled=True)
    return lax.psum_scatter(
        lax.dot_general(
            full_rows, coupling, (((0,), (0,)), ((), ())), preferred_element_type=jnp.float32
        ),
        "row",
        scatter_dimension=0,
        tiled=True,
    )


def solution(mesh):
    placed = (P("row", "col"), P(("freq", "row")))
    return jax.shard_map(
        on_device, mesh=mesh, in_specs=placed, out_specs=P(("freq", "row"), "col"), check_vma=False
    )
```

profile of v0, /device:TPU:0, one launch (start us, length us, event | category | flops | bytes accessed | tf_op | source)
XLA Modules:
  0.0 702.4 jit_solution(10874687154043378415)
XLA Ops:
  6.5 0.0 all-gather.2.cloned.1.call-start
  6.5 5.4 multiply_convert_fusion
  11.9 0.0 all-gather.2.cloned.1.call-update
  11.9 0.0 reduce-scatter.2.cloned.1.call-start
  12.0 325.4 %all-gather.2.cloned.1.call-done = bf16[1536,6144]{1,0:T(8,128)(2,1)} async-done(((bf16[1536,1536]{1,0:T(8,128)(2,1)}), bf16[1536,6144]{1,0:T(8,128)(2,1)}) %all-gather.2.cloned.1.call-update) | async-done | bytes 18874384 | tf_op jit(solution)/shard_map/all_gather | solution.py:9
  337.4 36.7 %fusion = f32[6144,1536]{1,0:T(8,128)} fusion(bf16[1536,6144]{1,0:T(8,128)(2,1)} %all-gather.2.cloned.1.call-done, bf16[1536,1536]{1,0:T(8,128)(2,1)} %param.2), kind=kOutput, calls=%fused_computation.1 | convolution fusion | flops 28991029248 | bytes 61341696 | tf_op jit(solution)/shard_map/dot_general | solution.py:11
  374.1 0.0 reduce-scatter.2.cloned.1.call-update
  374.1 321.4 %reduce-scatter.2.cloned.1.call-done = f32[1536,1536]{1,0:T(8,128)} async-done(((f32[6144,1536]{1,0:T(8,128)}), f32[1536,1536]{1,0:T(8,128)}) %reduce-scatter.2.cloned.1.call-update) | async-done | bytes 9437200 | tf_op jit(solution)/shard_map/reduce_scatter | solution.py:10
Async XLA Ops:
  6.5 330.8 %all-gather.2.cloned.1.call-start = ((), (), s32[]{:S(2)}) async-start(), calls=%async_computation.1 | async-start | bytes 23592960 | tf_op jit(solution)/shard_map/all_gather | solution.py:9
  11.9 683.6 %reduce-scatter.2.cloned.1.call-start = ((), (), s32[]{:S(2)}) async-start(), calls=%async_computation.2 | async-start | bytes 47185920 | tf_op jit(solution)/shard_map/reduce_scatter | solution.py:10
Sparse Core Ops, SparseCore 0:
  12.0 325.2 all-gather.1
  374.2 321.2 reduce-scatter.1
where the time goes:
time: 703 us; the launch traced here: 702 us
  waiting for transfers between devices  647 us (92%)
  matrix products  36.7 us (5%)
  between operations  13.4 us (2%)
    all_gather x1, waiting for transfers between devices, on_device(): full_rows = lax.all_gather(weighted, 'col', axis=1, tiled=True)  325 us
    reduce_scatter x1, waiting for transfers between devices, on_device(): lax.psum_scatter(lax.dot_general(full_rows, coupling, (((0,), (0,)), ((),...  321 us
    dot_general x1, matrix products, on_device(): lax.dot_general(full_rows, coupling, (((0,), (0,)), ((), ())), preferred_...  36.7 us
  transfers between devices with their start and end apart: 2, of which 2 were waited for; matrix products, arithmetic and copies ran while one was open for 0% of the time, Pallas kernels for 0%

commit v1 on v0

--- a/solution.py
+++ b/solution.py
@@ -6,7 +6,12 @@
 
 def on_device(coupling, freq_weight):
     weighted = (coupling.astype(jnp.float32) * freq_weight[:, None]).astype(jnp.bfloat16)
-    full_rows = lax.all_gather(weighted, "col", axis=1, tiled=True)
+    ring = [weighted]
+    for hop in range(3):
+        ring.append(lax.ppermute(ring[-1], "col", [(dev, (dev + 1) % 4) for dev in range(4)]))
+    full_rows = jnp.roll(
+        jnp.concatenate(ring[::-1], axis=1), (lax.axis_index("col") + 1) * ring[0].shape[1], axis=1
+    )
     return lax.psum_scatter(
         lax.dot_general(
             full_rows, coupling, (((0,), (0,)), ((), ())), preferred_element_type=jnp.float32

time: 703 us -> 723 us (1.028)
  local copies, waits for them, and re-layouts: 0 us -> 26.7 us
  waiting for transfers between devices: 647 us -> 633 us
    all_gather x1 -> x0, waiting for transfers between devices: 325 us -> none  [on_device(): full_rows = lax.all_gather(weighted, 'col', axis=1, tiled=True)]
    ppermute x0 -> x3, waiting for transfers between devices: none -> 313 us  [on_device(): lax.ppermute(ring[-1], 'col', [(dev, (dev + 1) % 4) for dev in range(4)])]
    unnamed x0 -> x18, local copies, waits for them, and re-layouts: none -> 26.7 us
  transfers between devices with their start and end apart: 2 -> 4, of which waited for: 2 -> 4; matrix products, arithmetic and copies ran while one was open for 0% -> 0% of each run, Pallas kernels for 0% -> 0%
where the time goes in v1:
time: 723 us
  waiting for transfers between devices  633 us (88%)
  matrix products  37 us (5%)
  local copies, waits for them, and re-layouts  26.7 us (4%)
  between operations  13.4 us (2%)
  other arithmetic  9.41 us (1%)
    reduce_scatter x1, waiting for transfers between devices, on_device(): lax.psum_scatter(lax.dot_general(full_rows, coupling, (((0,), (0,)), ((),...  320 us
    ppermute x3, waiting for transfers between devices, on_device(): lax.ppermute(ring[-1], 'col', [(dev, (dev + 1) % 4) for dev in range(4)])  313 us
    dot_general x1, matrix products, on_device(): lax.dot_general(full_rows, coupling, (((0,), (0,)), ((), ())), preferred_...  37 us
    unnamed x18, local copies, waits for them, and re-layouts  26.7 us
  transfers between devices with their start and end apart: 4, of which 4 were waited for; matrix products, arithmetic and copies ran while one was open for 0% of the time, Pallas kernels for 0%

profile of v1, /device:TPU:0, one launch (start us, length us, event | category | flops | bytes accessed | tf_op | source)
XLA Modules:
  0.0 722.9 jit_solution(16285318171752467127)
XLA Ops:
  6.5 0.0 slice-start
  6.5 0.0 copy-start.1
  6.5 0.0 reduce-scatter.2.cloned.1.call-start
  6.5 3.2 multiply_convert_fusion
  9.8 3.1 collective-permute-start
  12.9 103.8 %collective-permute-done = bf16[1536,1536]{1,0:T(8,128)(2,1)S(1)} collective-permute-done((bf16[1536,1536]{1,0:T(8,128)(2,1)S(1)}, bf16[1536,1536]{1,0:T(8,128)(2,1)S(1)}, u32[]{:S(2)}, u32[]{:S(2)}) %collective-permute-start) | collective-permute-done | bytes 4718624 | tf_op jit(solution)/shard_map/ppermute | solution.py:11
  116.7 0.0 copy-start
  116.7 2.2 copy-done
  118.9 0.0 collective-permute-start.1
  118.9 104.9 %collective-permute-done.1 = bf16[1536,1536]{1,0:T(8,128)(2,1)} collective-permute-done((bf16[1536,1536]{1,0:T(8,128)(2,1)S(1)}, bf16[1536,1536]{1,0:T(8,128)(2,1)}, u32[]{:S(2)}, u32[]{:S(2)}) %collective-permute-start.1) | collective-permute-done | bytes 4718624 | tf_op jit(solution)/shard_map/ppermute | solution.py:11
  223.8 0.0 collective-permute-start.2
  223.8 0.0 slice-start.2
  223.8 0.0 slice-start.1
  223.8 104.2 %collective-permute-done.2 = bf16[1536,1536]{1,0:T(8,128)(2,1)} collective-permute-done((bf16[1536,1536]{1,0:T(8,128)(2,1)}, bf16[1536,1536]{1,0:T(8,128)(2,1)}, u32[]{:S(2)}, u32[]{:S(2)}) %collective-permute-start.2) | collective-permute-done | bytes 4718624 | tf_op jit(solution)/shard_map/ppermute | solution.py:11
  328.0 4.8 constant_dynamic-update-slice_fusion.7
  332.9 0.0 slice-start.3
  332.9 5.0 constant_dynamic-update-slice_fusion.6
  337.8 0.0 slice-done.2
  337.8 0.0 slice-done.3
  337.8 2.5 constant_dynamic-update-slice_fusion.5
  340.4 0.0 slice-done
  340.4 0.0 copy-done.1
  340.4 0.0 slice-done.1
  340.4 3.0 constant_dynamic-update-slice_fusion.4
  343.4 4.8 constant_dynamic-update-slice_fusion.3
  348.2 4.8 constant_dynamic-update-slice_fusion.2
  353.1 2.5 constant_dynamic-update-slice_fusion.1
  355.6 3.1 constant_dynamic-update-slice_fusion
  358.7 37.0 %fusion = f32[6144,1536]{1,0:T(8,128)} fusion(bf16[1536,1536]{1,0:T(8,128)(2,1)S(1)} %bitcast.2, bf16[1536,12288]{1,0:T(8,128)(2,1)} %constant_dynamic-update-slice_fusion, s32[]{:T(128)S(6)} %select_n.14), kind=kOutput, calls=%fused_computation | convolution fusion | flops 28991029248 | bytes 61341700 | tf_op jit(solution)/shard_map/dot_general | solution.py:16
  395.7 0.0 reduce-scatter.2.cloned.1.call-update
  395.8 320.3 %reduce-scatter.2.cloned.1.call-done = f32[1536,1536]{1,0:T(8,128)} async-done(((f32[6144,1536]{1,0:T(8,128)}), f32[1536,1536]{1,0:T(8,128)}) %reduce-scatter.2.cloned.1.call-update) | async-done | bytes 9437200 | tf_op jit(solution)/shard_map/reduce_scatter | solution.py:15
  (2 shorter events, 0.0 us)
Async XLA Ops:
  6.5 333.8 %slice-start = ((s8[4718592]{0:T(1024)(128)(4,1)}), s8[524288]{0:T(1024)(128)(4,1)S(1)}, s32[]{:S(2)}) async-start(s8[4718592]{0:T(1024)(128)(4,1)} %bitcast.1), calls=%async_computation.2 | async-start | bytes 1048576
  6.5 333.8 %copy-start.1 = (f32[1536]{0:T(1024)S(1)}, f32[1536]{0:T(1024)}, u32[]{:S(2)}) copy-start(f32[1536]{0:T(1024)} %param.3) | copy-start | bytes 18436
  6.5 709.5 %reduce-scatter.2.cloned.1.call-start = ((), (), s32[]{:S(2)}) async-start(), calls=%async_computation.1 | async-start | bytes 47185920 | tf_op jit(solution)/shard_map/reduce_scatter | solution.py:15
  9.8 106.9 %collective-permute-start = (bf16[1536,1536]{1,0:T(8,128)(2,1)S(1)}, bf16[1536,1536]{1,0:T(8,128)(2,1)S(1)}, u32[]{:S(2)}, u32[]{:S(2)}) collective-permute-start(bf16[1536,1536]{1,0:T(8,128)(2,1)S(1)} %multiply_convert_fusion), channel_id=1, source_target_pairs={{0,1},{1,2},{2,3},{3,0},{4,5},{5,6},{6,7},{7,4},{8,9},{9,10},{10,1... | collective-permute-start | bytes 14155784 | tf_op jit(solution)/shard_map/ppermute | solution.py:11
  116.7 2.2 copy-start
  118.9 104.9 %collective-permute-start.1 = (bf16[1536,1536]{1,0:T(8,128)(2,1)S(1)}, bf16[1536,1536]{1,0:T(8,128)(2,1)}, u32[]{:S(2)}, u32[]{:S(2)}) collective-permute-start(bf16[1536,1536]{1,0:T(8,128)(2,1)S(1)} %collective-permute-done), channel_id=1, source_target_pairs={{0,1},{1,2},{2,3},{3,0},{4,5},{5,6},{6,7},{7,4},{8,9},{9,10},{10,1... | collective-permute-start | bytes 14155784 | tf_op jit(solution)/shard_map/ppermute | solution.py:11
  223.8 104.2 %collective-permute-start.2 = (bf16[1536,1536]{1,0:T(8,128)(2,1)}, bf16[1536,1536]{1,0:T(8,128)(2,1)}, u32[]{:S(2)}, u32[]{:S(2)}) collective-permute-start(bf16[1536,1536]{1,0:T(8,128)(2,1)} %collective-permute-done.1), channel_id=1, source_target_pairs={{0,1},{1,2},{2,3},{3,0},{4,5},{5,6},{6,7},{7,4},{8,9},{9,10},{10,1... | collective-permute-start | bytes 14155784 | tf_op jit(solution)/shard_map/ppermute | solution.py:11
  223.8 114.0 %slice-start.2 = ((s8[4718592]{0:T(1024)(128)(4,1)}), s8[4194304]{0:T(1024)(128)(4,1)S(1)}, s32[]{:S(2)}) async-start(s8[4718592]{0:T(1024)(128)(4,1)} %bitcast.3), calls=%async_computation.4 | async-start | bytes 8388608
  223.8 116.6 %slice-start.1 = ((s8[4718592]{0:T(1024)(128)(4,1)}), s8[4194304]{0:T(1024)(128)(4,1)S(1)}, s32[]{:S(2)}) async-start(s8[4718592]{0:T(1024)(128)(4,1)} %bitcast.1), calls=%async_computation.3 | async-start | bytes 8388608
  332.9 5.0 slice-start.3
Sparse Core Ops, SparseCore 0:
  395.9 320.1 reduce-scatter.1
